TPU v7x, 32 devices: a whole 2x2x4 slice. The times are simulated.
32 devices in a mesh: lb: 4 (over z), rb: 4 (over y, x), wa: 2 (over core).
Axes of the slice: x: 2, y: 2, z: 4, core: 2. Of those that a mesh axis runs over, the one named last changes fastest.
Arguments:
- initial_guess: bfloat16 [8192, 4, 128], P(('lb', 'rb')), may hold values from -6 to 6
- left_environment: bfloat16 [8, 4, 4, 512, 8192], P('wa', None, 'rb', None, 'lb'), may hold values from -12 to 12, as said below
- right_environment: bfloat16 [128, 8, 128], replicated, may hold values from -12 to 12, as said below
- operator_blocks: float32 [16, 4, 4], replicated, may hold values from -4 to 4
- operator_pairs: int32 [16, 2], replicated, may hold values from 0 to 7
Outputs:
- ritz_vector: float32 [8192, 4, 128], P(('lb', 'rb'))
- residual: float32 [8192, 4, 128], P(('lb', 'rb'))
Inputs may be any that keep to these rules, and one draw needn't show every extreme that they name: `operator_pairs`: each row names the left and the right MPO index of one operator block; blocks with the same pair add. `left_environment`: for each MPO index the [8192, 8192] matrix is symmetric. `right_environment`: for each MPO index the matrix over the two right bond states is symmetric.
All inputs are finite; a program needn't handle non-finite values.
Results may differ from a plain program's by a relative error of at most 0.014.
Values may be sent and summed in bfloat16 or wider, within the bound.
A program may use at most 192 MiB of HBM per device.

v0:
```python
import functools

import jax
import jax.numpy as jnp
from jax import lax
from jax.experimental import pallas as pl
from jax.experimental.pallas import tpu as pltpu
from jax.sharding import PartitionSpec as P

ITERS = 3
SWEEPS = 8

highest = lax.Precision.HIGHEST
epsilon = 1e-06

TILE = (8, 128)
LANES = 128
VMEM_BYTES = 66_000_000
MESH_IDS = pl.DeviceIdType.MESH


def half_angle(y, x):
    scale = jnp.maximum(jnp.abs(x), jnp.abs(y))
    zero = scale == 0.0
    inverse = 1.0 / jnp.where(zero, 1.0, scale)
    xs, ys = x * inverse, y * inverse
    h = jnp.sqrt(xs * xs + ys * ys)
    h = jnp.where(zero, 1.0, h)
    big = jnp.sqrt(0.5 * (1.0 + jnp.abs(xs) / h))
    small = 0.5 * jnp.abs(ys) / (h * big)
    positive = x >= 0.0
    cosine = jnp.where(positive, big, small)
    sine = jnp.where(positive, small, big) * jnp.where(y < 0.0, -1.0, 1.0)
    return jnp.where(zero, 1.0, cosine), jnp.where(zero, 0.0, sine)


def lowest_pair(order, entry):
    def at(i, j):
        return (min(i, j), max(i, j))

    one, none = jnp.full(TILE, 1.0, jnp.float32), jnp.full(TILE, 0.0, jnp.float32)
    if order == 1:
        return entry(0, 0), [one]
    keys = [(i, j) for i in range(order) for j in range(i, order)]
    start = tuple(entry(i, j) for i, j in keys)
    vectors0 = tuple(one if i == j else none for i in range(order) for j in range(order))

    def sweep(_, carry):
        m = dict(zip(keys, carry[0]))
        v = list(carry[1])
        for p in range(order):
            for q in range(p + 1, order):
                a, b, d = m[(p, p)], m[(p, q)], m[(q, q)]
                c, s = half_angle(2.0 * b, d - a)
                m[(p, p)] = c * (c * a - s * b) - s * (c * b - s * d)
                m[(p, q)] = s * (c * a - s * b) + c * (c * b - s * d)
                m[(q, q)] = s * (s * a + c * b) + c * (s * b + c * d)
                for i in range(order):
                    if i != p and i != q:
                        x, y = m[at(i, p)], m[at(i, q)]
                        m[at(i, p)] = c * x - s * y
                        m[at(i, q)] = s * x + c * y
                    x, y = v[i * order + p], v[i * order + q]
                    v[i * order + p] = c * x - s * y
                    v[i * order + q] = s * x + c * y
        return tuple(m[key] for key in keys), tuple(v)

    values, vectors = lax.fori_loop(0, SWEEPS, sweep, (start, vectors0))
    m = dict(zip(keys, values))
    best = m[(0, 0)]
    weights = [vectors[i * order] for i in range(order)]
    for j in range(1, order):
        better = m[(j, j)] < best
        best = jnp.where(better, m[(j, j)], best)
        weights = [
            jnp.where(better, vectors[i * order + j], weights[i]) for i in range(order)
        ]
    sign = jnp.where(weights[0] < 0.0, -1.0, 1.0)
    return best, [weight * sign for weight in weights]


def dense_operator(operator_blocks, operator_pairs, levels):
    symmetric = 0.5 * (operator_blocks + jnp.swapaxes(operator_blocks, 1, 2))
    indices = jnp.arange(levels, dtype=jnp.int32)
    left_hot = (operator_pairs[:, 0:1] == indices[None, :]).astype(jnp.float32)
    right_hot = (operator_pairs[:, 1:2] == indices[None, :]).astype(jnp.float32)
    return jnp.einsum("nw,nv,nts->wvts", left_hot, right_hot, symmetric, precision=highest)


def fold(block):
    rows, columns = block.shape
    total = None
    for r in range(0, rows, TILE[0]):
        for c in range(0, columns, LANES):
            piece = block[r : r + TILE[0], c : c + LANES]
            total = piece if total is None else total + piece
    return total


def scalar_of(tile):
    return tile[0:1, 0:1]


def davidson_kernel(
    dims,
    op_ref, guess_ref, right_ref, left_hbm,
    vec_out, res_out,
    left, joint, xall, inner, wsend, wrecv, zsend, zrecv,
    basis, images, diag, vec, img, rows_ref, dots, sub, pair,
    load_sem, gx_send, gx_recv, gw_send, gw_recv, w_send, w_recv, z_send, z_recv,
    d_sem, dot_send, dot_recv, out_sem,
):
    (n_lb, n_rb, n_wa, rb_minor, own_rows, half, width, window, physical, levels,
     local_levels, total_count) = dims
    devices = n_lb * n_rb * n_wa
    i, j, w = lax.axis_index("lb"), lax.axis_index("rb"), lax.axis_index("wa")
    me = (i * n_rb + j) * n_wa + w
    other = 1 - w
    partner = (i, j, other)
    chunk = min(32, half)
    rb_major = n_rb // rb_minor

    def device_of(flat):
        return (
            lax.div(flat, n_rb * n_wa),
            lax.rem(lax.div(flat, n_wa), n_rb),
            lax.rem(flat, n_wa),
        )

    def rb_step(step, sign):
        high, low = lax.div(j, rb_minor), lax.rem(j, rb_minor)
        dh, dl = lax.div(step, rb_minor), lax.rem(step, rb_minor)
        if sign > 0:
            high, low = lax.rem(high + dh, rb_major), lax.rem(low + dl, rb_minor)
        else:
            high = lax.rem(high - dh + rb_major, rb_major)
            low = lax.rem(low - dl + rb_minor, rb_minor)
        return high * rb_minor + low

    def remote(src, dst, send, recv, target):
        return pltpu.make_async_remote_copy(
            src_ref=src, dst_ref=dst, send_sem=send, recv_sem=recv,
            device_id=target, device_id_type=MESH_IDS,
        )

    def rows_at(index, size=chunk):
        return pl.ds(pl.multiple_of(index, size), size)

    def over_chunks(body, init):
        return lax.fori_loop(0, half // chunk, body, init)

    barrier = pltpu.get_barrier_semaphore()

    def greet(step, carry):
        target = device_of(lax.rem(me + step, devices))
        pl.semaphore_signal(barrier, inc=1, device_id=target, device_id_type=MESH_IDS)
        return carry

    lax.fori_loop(1, devices, greet, 0)

    def target_block(t):
        return lax.rem(i + 1 + t, n_lb)

    def load_block(t):
        span = pl.ds(pl.multiple_of(target_block(t) * own_rows, own_rows), own_rows)
        return pltpu.make_async_copy(
            left_hbm.at[:, span, :], left.at[:, span, :], load_sem.at[t]
        )

    for t in range(n_lb):
        load_block(t).start()

    xall[j, w] = guess_ref[...]

    def prepare(c, carry):
        at = rows_at(c * chunk)
        vec[at, :] = guess_ref[at, :].astype(jnp.float32)
        zeros = jnp.zeros((chunk, width), jnp.float32)
        for n in range(ITERS):
            basis[n, at, :] = zeros
            images[n, at, :] = zeros
        return carry

    over_chunks(prepare, 0)
    pl.semaphore_wait(barrier, devices - 1)

    def gather_rb(step):
        q = rb_step(step, 1)
        return remote(
            xall.at[j, w], xall.at[j, w], gx_send.at[step], gx_recv.at[step], (i, q, w)
        )

    def gather_wa(step):
        q = rb_step(step, -1)
        return remote(xall.at[q, w], xall.at[q, w], gw_send.at[step], gw_recv.at[step], partner)

    def send_vector():
        gather_wa(0).start()
        for step in range(1, n_rb):
            gather_rb(step).start()

    send_vector()

    op_base = w * (local_levels * levels * physical * physical)
    band = min(32, window)

    def make_joint(index, carry):
        k = lax.div(index, window // band)
        r0 = lax.rem(index, window // band) * band
        mats = [right_ref[v, pl.ds(pl.multiple_of(r0, band), band), :] for v in range(levels)]
        for s in range(physical):
            for t in range(physical):
                total = None
                for v in range(levels):
                    at = op_base + ((k * levels + v) * physical + t) * physical + s
                    term = op_ref[at] * mats[v]
                    total = term if total is None else total + term
                high = total.astype(jnp.bfloat16)
                low = (total - high.astype(jnp.float32)).astype(jnp.bfloat16)
                rows = pl.ds(pl.multiple_of(s * window + r0, band), band)
                joint[k, 0, rows, t * window : (t + 1) * window] = high
                joint[k, 1, rows, t * window : (t + 1) * window] = low
        return carry

    lax.fori_loop(0, local_levels * (window // band), make_joint, 0)

    eye = lax.broadcasted_iota(jnp.int32, (window, window), 0) == lax.broadcasted_iota(
        jnp.int32, (window, window), 1
    )
    right_diag = [
        jnp.sum(jnp.where(eye, right_ref[v], 0.0), axis=0, keepdims=True) for v in range(levels)
    ]
    for k in range(local_levels):
        for s in range(physical):
            total = None
            for v in range(levels):
                at = op_base + ((k * levels + v) * physical + s) * physical + s
                term = op_ref[at] * right_diag[v]
                total = term if total is None else total + term
            rows_ref[k, :, s * window : (s + 1) * window] = total

    def diagonal_part(r0):
        first = j * own_rows + r0
        base = lax.div(first, LANES) * LANES
        shift = first - base
        lane = lax.broadcasted_iota(jnp.int32, (chunk, LANES), 1)
        row = lax.broadcasted_iota(jnp.int32, (chunk, LANES), 0)
        mask = lane == row + shift
        total = None
        for k in range(local_levels):
            block = left[
                k,
                pl.ds(pl.multiple_of(i * own_rows + r0, chunk), chunk),
                pl.ds(pl.multiple_of(base, LANES), LANES),
            ].astype(jnp.float32)
            column = jnp.sum(jnp.where(mask, block, 0.0), axis=1, keepdims=True)
            term = column * rows_ref[k]
            total = term if total is None else total + term
        return total

    def all_reduce(slot, tiles):
        rows = [jnp.sum(tile, axis=0, keepdims=True) for tile in tiles]
        lane8 = lax.broadcasted_iota(jnp.int32, TILE, 1)
        row8 = lax.broadcasted_iota(jnp.int32, TILE, 0)
        stacked = jnp.zeros(TILE, jnp.float32)
        for n, row in enumerate(rows):
            stacked = jnp.where(row8 == n, row, stacked)
        column = jnp.sum(stacked, axis=1, keepdims=True)
        line = jnp.sum(jnp.where(lane8 == row8, column, 0.0), axis=0, keepdims=True)
        dots[slot, me] = line

        def send(step, carry):
            target = device_of(lax.rem(me + step, devices))
            remote(
                dots.at[slot, me], dots.at[slot, me], dot_send.at[slot], dot_recv.at[slot], target
            ).start()
            return carry

        lax.fori_loop(1, devices, send, 0)
        most = dots.at[slot, pl.ds(0, devices - 1)]
        pltpu.make_async_copy(most, most, dot_send.at[slot]).wait()
        pltpu.make_async_copy(most, most, dot_recv.at[slot]).wait()
        total = jnp.sum(dots[slot], axis=0)
        spread = jnp.sum(jnp.where(lane8 == row8, total, 0.0), axis=1, keepdims=True)
        spread = spread * (1.0 / total_count)
        return [jnp.broadcast_to(spread[n : n + 1, :], TILE) for n in range(len(tiles))]

    def inner_block(q, u):
        x = xall[q, u]
        at = pl.ds(pl.multiple_of(q * own_rows + u * half, half), half)

        def one(k, carry):
            value = jnp.dot(x, joint[k, 0], preferred_element_type=jnp.float32)
            value = value + jnp.dot(x, joint[k, 1], preferred_element_type=jnp.float32)
            inner[k, at, :] = value.astype(jnp.bfloat16)
            return carry

        lax.fori_loop(0, local_levels, one, 0)

    def rows_times(block, u):
        at = pl.ds(pl.multiple_of(block * own_rows + u * half, half), half)
        total = None
        for k in range(local_levels):
            term = jnp.dot(left[k, at, :], inner[k], preferred_element_type=jnp.float32)
            total = term if total is None else total + term
        return total

    def exchange(t):
        return remote(wsend.at[t], wrecv.at[t], w_send.at[t], w_recv.at[t], partner)

    def scatter(t):
        return remote(
            zsend.at[t], zrecv.at[t], z_send.at[t], z_recv.at[t], (target_block(t), j, w)
        )

    def iteration(it, carry):
        inner_block(j, w)
        gather_wa(0).wait_recv()
        inner_block(j, other)

        def arrive(step, c):
            q = rb_step(step, -1)
            gather_rb(step).wait_recv()
            gather_wa(step).start()
            inner_block(q, w)
            gather_wa(step).wait_recv()
            inner_block(q, other)
            return c

        lax.fori_loop(1, n_rb, arrive, 0)

        def block_sum(t):
            block = target_block(t)

            @pl.when(it == 0)
            def _():
                load_block(t).wait()

            wsend[t] = rows_times(block, other)
            exchange(t).start()
            value = rows_times(block, w)
            exchange(t).wait_recv()
            return value + wrecv[t]

        def away(t, c):
            zsend[t] = block_sum(t).astype(jnp.bfloat16)
            scatter(t).start()
            return c

        lax.fori_loop(0, n_lb - 1, away, 0)
        img[...] = block_sum(n_lb - 1)

        @pl.when(it == 0)
        def _():
            def mine(c, carry):
                diag[rows_at(c * chunk), :] = diagonal_part(w * half + c * chunk)
                return carry

            def theirs(c, carry):
                images[ITERS, rows_at(c * chunk), :] = diagonal_part(other * half + c * chunk)
                return carry

            over_chunks(theirs, 0)
            swap = remote(images.at[ITERS], basis.at[ITERS], d_sem.at[0], d_sem.at[1], partner)
            swap.start()
            over_chunks(mine, 0)
            swap.wait()

            def join(c, carry):
                at = rows_at(c * chunk)
                diag[at, :] = diag[at, :] + basis[ITERS, at, :]
                return carry

            over_chunks(join, 0)

        gather_wa(0).wait_send()
        for step in range(1, n_rb):
            gather_rb(step).wait_send()
            gather_wa(step).wait_send()
        for t in range(n_lb):
            exchange(t).wait_send()
        for t in range(n_lb - 1):
            scatter(t).wait_send()
        for t in range(n_lb - 1):
            scatter(t).wait_recv()

        def measure(c, sums):
            at = rows_at(c * chunk)
            y = img[at, :]
            for t in range(n_lb - 1):
                y = y + zrecv[t, at, :].astype(jnp.float32)
            img[at, :] = y
            x = vec[at, :]
            parts = [x * x, x * y] + [basis[n, at, :] * y for n in range(ITERS)]
            return tuple(total + fold(part) for total, part in zip(sums, parts))

        zero = jnp.zeros(TILE, jnp.float32)
        sums = over_chunks(measure, (zero,) * (2 + ITERS))
        sums = all_reduce(1, sums)
        scale = lax.rsqrt(sums[0] + epsilon)

        def keep(c, carry):
            at = rows_at(c * chunk)
            basis[it, at, :] = vec[at, :] * scalar_of(scale)
            images[it, at, :] = img[at, :] * scalar_of(scale)
            return carry

        over_chunks(keep, 0)

        for order in range(1, ITERS + 2):

            @pl.when(it == order - 1)
            def _():
                last = order - 1
                for n in range(last):
                    sub[n * (ITERS + 1) + last] = sums[2 + n] * scale
                sub[last * (ITERS + 1) + last] = sums[1] * scale * scale
                value, weights = lowest_pair(order, lambda a, b: sub[a * (ITERS + 1) + b])
                pair[0] = value
                for n in range(ITERS + 1):
                    pair[n + 1] = weights[n] if n < order else zero

        def ritz(at, members):
            value = scalar_of(pair[0])
            weight = [scalar_of(pair[n + 1]) for n in range(members)]
            u = weight[0] * basis[0, at, :]
            r = weight[0] * images[0, at, :]
            for n in range(1, members):
                u = u + weight[n] * basis[n, at, :]
                r = r + weight[n] * images[n, at, :]
            return value, u, r - value * u

        @pl.when(it < ITERS)
        def _():
            def correct(c, sums):
                at = rows_at(c * chunk)
                value, _, r = ritz(at, ITERS)
                x = r / (jnp.abs(diag[at, :] - value) + 1.0)
                vec[at, :] = x
                return tuple(
                    total + fold(basis[n, at, :] * x) for n, total in enumerate(sums)
                )

            overlaps = all_reduce(0, over_chunks(correct, (zero,) * ITERS))

            def project(c, carry):
                at = rows_at(c * chunk)
                x = vec[at, :]
                total = scalar_of(overlaps[0]) * basis[0, at, :]
                for n in range(1, ITERS):
                    total = total + scalar_of(overlaps[n]) * basis[n, at, :]
                x = x - total
                vec[at, :] = x
                xall[j, w, at, :] = x.astype(jnp.bfloat16)
                return carry

            over_chunks(project, 0)
            send_vector()

        @pl.when(it == ITERS)
        def _():
            def finish(c, carry):
                at = rows_at(c * chunk)
                _, u, r = ritz(at, ITERS + 1)
                vec[at, :] = u
                img[at, :] = r
                return carry

            over_chunks(finish, 0)
            span = pl.ds(pl.multiple_of(w * half, half), half)
            moves = []
            for n, (src, dst) in enumerate(((vec, vec_out), (img, res_out))):
                moves.append(
                    remote(src, dst.at[span, :], out_sem.at[3 * n], out_sem.at[3 * n + 1], partner)
                )
                moves.append(pltpu.make_async_copy(src, dst.at[span, :], out_sem.at[3 * n + 2]))
            for move in moves:
                move.start()
            for move in moves:
                move.wait()

        return carry

    lax.fori_loop(0, ITERS + 1, iteration, 0)


def minor_of(size):
    best = 1
    for candidate in range(1, size + 1):
        if candidate * candidate <= size and size % candidate == 0:
            best = candidate
    return best


def per_device(initial_guess, left_environment, right_environment, operator_blocks, operator_pairs):
    own_rows, physical, window = initial_guess.shape
    width = physical * window
    levels = right_environment.shape[1]
    local_levels, coarse = left_environment.shape[:2]
    contracted = left_environment.shape[4]
    n_lb, n_rb, n_wa = lax.axis_size("lb"), lax.axis_size("rb"), lax.axis_size("wa")
    half = own_rows // n_wa
    total_count = own_rows * physical * window * n_lb * n_rb
    devices = n_lb * n_rb * n_wa

    operator = dense_operator(operator_blocks, operator_pairs, levels).reshape(-1)
    right = jnp.transpose(right_environment, (1, 0, 2)).astype(jnp.float32)
    left_matrix = left_environment.reshape(local_levels, coarse * own_rows, contracted)
    guess = lax.dynamic_slice_in_dim(initial_guess, lax.axis_index("wa") * half, half, 0)
    guess = guess.reshape(half, width)

    dims = (n_lb, n_rb, n_wa, minor_of(n_rb), own_rows, half, width, window, physical, levels,
            local_levels, total_count)
    f32, bf16 = jnp.float32, jnp.bfloat16
    members = ITERS + 1
    dma = pltpu.SemaphoreType.DMA
    outs = jax.ShapeDtypeStruct((own_rows, width), f32)
    vmem = pl.BlockSpec(memory_space=pltpu.VMEM)
    hbm = pl.BlockSpec(memory_space=pl.ANY)
    vectors, residuals = pl.pallas_call(
        functools.partial(davidson_kernel, dims),
        out_shape=(outs, outs),
        in_specs=[pl.BlockSpec(memory_space=pltpu.SMEM), vmem, vmem, hbm],
        out_specs=(hbm, hbm),
        scratch_shapes=[
            pltpu.VMEM((local_levels, coarse * own_rows, contracted), bf16),
            pltpu.VMEM((local_levels, 2, width, width), bf16),
            pltpu.VMEM((n_rb, n_wa, half, width), bf16),
            pltpu.VMEM((local_levels, contracted, width), bf16),
            pltpu.VMEM((n_lb, half, width), f32),
            pltpu.VMEM((n_lb, half, width), f32),
            pltpu.VMEM((n_lb - 1, half, width), bf16),
            pltpu.VMEM((n_lb - 1, half, width), bf16),
            pltpu.VMEM((members, half, width), f32),
            pltpu.VMEM((members, half, width), f32),
            pltpu.VMEM((half, width), f32),
            pltpu.VMEM((half, width), f32),
            pltpu.VMEM((half, width), f32),
            pltpu.VMEM((local_levels, 1, width), f32),
            pltpu.VMEM((2, devices, 1, LANES), f32),
            pltpu.VMEM((members * members,) + TILE, f32),
            pltpu.VMEM((members + 1,) + TILE, f32),
            dma((n_lb,)),
            dma((n_rb,)),
            dma((n_rb,)),
            dma((n_rb,)),
            dma((n_rb,)),
            dma((n_lb,)),
            dma((n_lb,)),
            dma((n_lb,)),
            dma((n_lb,)),
            dma((2,)),
            dma((2,)),
            dma((2,)),
            dma((6,)),
        ],
        compiler_params=pltpu.CompilerParams(
            collective_id=0, has_side_effects=True, vmem_limit_bytes=VMEM_BYTES
        ),
        name="davidson",
    )(operator, guess, right, left_matrix)

    shape = (own_rows, physical, window)
    return vectors.reshape(shape), residuals.reshape(shape)


def solution(mesh):
    in_specs = (P(("lb", "rb"), None, None), P("wa", None, "rb", None, "lb"), P(), P(), P())
    out_specs = (P(("lb", "rb"), None, None), P(("lb", "rb"), None, None))
    return jax.shard_map(
        per_device, mesh=mesh, in_specs=in_specs, out_specs=out_specs, check_vma=False
    )
```

profile of v0, /device:TPU:0, one launch (start us, length us, event | category | flops | bytes accessed | tf_op | source)
XLA Modules:
  0.0 255.4 jit_solution(3180792262095445816)
XLA Ops:
  0.6 0.0 copy-start
  0.6 0.8 slice_bitcast_fusion.1
  1.4 1.4 convolution_bitcast_fusion
  2.8 0.3 copy.10
  3.1 0.8 reshape.19.op_ref
  3.9 0.0 copy-done
  3.9 0.1 constant_dynamic-slice_fusion
  4.0 0.7 copy.20
  4.7 1.8 convert_bitcast_fusion.right_ref
  6.5 243.8 %davidson.1 = (f32[512,512]{1,0:T(8,128)}, f32[512,512]{1,0:T(8,128)}) custom-call(f32[1024]{0:T(1024)} %reshape.19.op_ref, bf16[256,512]{1,0:T(8,128)(2,1)} %bitcast.29, f32[8,128,128]{2,1,0:T(8,128)} %convert_bitcast_fusion.right_ref, bf16[4,2048,2048]{2,1,0:T(8,128)(2,1)} %bitcast.28), custom_call_target="tpu_custom_call" | custom-call | tf_op jit(solution)/shard_map/davidson/pallas_call | solution.py:520
  250.3 2.5 reshape.22
  252.8 2.5 reshape.23
  (1 shorter events, 0.0 us)
Async XLA Ops:
  0.6 3.2 %copy-start = (bf16[512,4,128]{2,1,0:T(4,128)(2,1)S(1)}, bf16[512,4,128]{2,1,0:T(4,128)(2,1)}, u32[]{:S(2)}) copy-start(bf16[512,4,128]{2,1,0:T(4,128)(2,1)} %param.5) | copy-start | bytes 1572868
where the time goes:
time: 256 us; the launch traced here: 255 us
  Pallas kernels  244 us (95%)
  local copies, waits for them, and re-layouts  7.69 us (3%)
    pallas_call x1, Pallas kernels, per_device(): pl.pallas_call(functools.partial(davidson_kernel, dims), out_shape=(outs,...  244 us

commit v1 on v0

--- a/solution.py
+++ b/solution.py
@@ -106,7 +106,7 @@
     op_ref, guess_ref, right_ref, left_hbm,
     vec_out, res_out,
     left, joint, xall, inner, wsend, wrecv, zsend, zrecv,
-    basis, images, diag, vec, img, rows_ref, dots, sub, pair,
+    basis, images, diag, vec, img, rows_ref, dots, sub, pair, over,
     load_sem, gx_send, gx_recv, gw_send, gw_recv, w_send, w_recv, z_send, z_recv,
     d_sem, dot_send, dot_recv, out_sem,
 ):
@@ -158,8 +158,19 @@
 
     lax.fori_loop(1, devices, greet, 0)
 
+    long_side = jnp.maximum(i, n_lb - 1 - i)
+    short_side = jnp.minimum(i, n_lb - 1 - i)
+    toward = jnp.where(2 * i <= n_lb - 1, 1, -1)
+    interior = jnp.logical_and(i > 0, i < n_lb - 1)
+
     def target_block(t):
-        return lax.rem(i + 1 + t, n_lb)
+        if t == n_lb - 1:
+            return i
+        rest = t - (long_side - short_side)
+        pair_at = jnp.maximum(rest, 0)
+        near = short_side - lax.div(pair_at, 2)
+        sign = jnp.where(lax.rem(pair_at, 2) == 0, -toward, toward)
+        return jnp.where(rest < 0, i + toward * (long_side - t), i + sign * near)
 
     def load_block(t):
         span = pl.ds(pl.multiple_of(target_block(t) * own_rows, own_rows), own_rows)
@@ -182,6 +193,17 @@
         return carry
 
     over_chunks(prepare, 0)
+    for n in range(ITERS):
+        over[n] = jnp.zeros(TILE, jnp.float32)
+
+    @pl.when(i == 0)
+    def _():
+        zrecv[i] = jnp.zeros((half, width), jnp.bfloat16)
+
+    @pl.when(i == n_lb - 1)
+    def _():
+        zrecv[n_lb] = jnp.zeros((half, width), jnp.bfloat16)
+
     pl.semaphore_wait(barrier, devices - 1)
 
     def gather_rb(step):
@@ -258,10 +280,11 @@
             total = term if total is None else total + term
         return total
 
-    def all_reduce(slot, tiles):
+    lane8 = lax.broadcasted_iota(jnp.int32, TILE, 1)
+    row8 = lax.broadcasted_iota(jnp.int32, TILE, 0)
+
+    def reduce_start(slot, tiles):
         rows = [jnp.sum(tile, axis=0, keepdims=True) for tile in tiles]
-        lane8 = lax.broadcasted_iota(jnp.int32, TILE, 1)
-        row8 = lax.broadcasted_iota(jnp.int32, TILE, 0)
         stacked = jnp.zeros(TILE, jnp.float32)
         for n, row in enumerate(rows):
             stacked = jnp.where(row8 == n, row, stacked)
@@ -277,13 +300,15 @@
             return carry
 
         lax.fori_loop(1, devices, send, 0)
+
+    def reduce_finish(slot, count):
         most = dots.at[slot, pl.ds(0, devices - 1)]
         pltpu.make_async_copy(most, most, dot_send.at[slot]).wait()
         pltpu.make_async_copy(most, most, dot_recv.at[slot]).wait()
         total = jnp.sum(dots[slot], axis=0)
         spread = jnp.sum(jnp.where(lane8 == row8, total, 0.0), axis=1, keepdims=True)
         spread = spread * (1.0 / total_count)
-        return [jnp.broadcast_to(spread[n : n + 1, :], TILE) for n in range(len(tiles))]
+        return [jnp.broadcast_to(spread[n : n + 1, :], TILE) for n in range(count)]
 
     def inner_block(q, u):
         x = xall[q, u]
@@ -305,18 +330,63 @@
             total = term if total is None else total + term
         return total
 
+    def rows_times_part(block, u, q):
+        at = pl.ds(pl.multiple_of(block * own_rows + u * half, half), half)
+        span = pl.ds(pl.multiple_of(q * own_rows, own_rows), own_rows)
+        total = None
+        for k in range(local_levels):
+            term = jnp.dot(
+                left[k, at, span], inner[k, span, :], preferred_element_type=jnp.float32
+            )
+            total = term if total is None else total + term
+        return total
+
     def exchange(t):
         return remote(wsend.at[t], wrecv.at[t], w_send.at[t], w_recv.at[t], partner)
 
-    def scatter(t):
+    def piece_rows(piece):
+        return pl.ds(piece * (half // 2), half // 2)
+
+    def scatter(t, piece):
+        block = target_block(t)
+        right = block > i
+        towards = jnp.where(right, i + 1, i - 1)
+        slot = jnp.where(block == i - 1, n_lb, block)
+        at = piece_rows(piece)
         return remote(
-            zsend.at[t], zrecv.at[t], z_send.at[t], z_recv.at[t], (target_block(t), j, w)
+            zsend.at[t, at], zrecv.at[slot, at], z_send.at[2 * t + piece],
+            z_recv.at[2 * slot + piece], (towards, j, w),
         )
 
+    def arrived(slot, piece):
+        at = piece_rows(piece)
+        return pltpu.make_async_copy(
+            zrecv.at[slot, at], zrecv.at[slot, at], z_recv.at[2 * slot + piece]
+        )
+
+    by_parts = own_rows % LANES == 0
+    units = 2 * (n_lb - 1)
+
     def iteration(it, carry):
+        def loaded(t):
+            @pl.when(it == 0)
+            def _():
+                load_block(t).wait()
+
+        first_block = target_block(0)
+        loaded(0)
+
+        def first_parts(q, start):
+            if not by_parts:
+                return
+            for u, dst in ((other, wsend.at[0]), (w, img)):
+                value = rows_times_part(first_block, u, q)
+                dst[...] = value if start else dst[...] + value
+
         inner_block(j, w)
         gather_wa(0).wait_recv()
         inner_block(j, other)
+        first_parts(j, True)
 
         def arrive(step, c):
             q = rb_step(step, -1)
@@ -325,30 +395,57 @@
             inner_block(q, w)
             gather_wa(step).wait_recv()
             inner_block(q, other)
+            first_parts(q, False)
             return c
 
         lax.fori_loop(1, n_rb, arrive, 0)
-
-        def block_sum(t):
+        if not by_parts:
+            wsend[0] = rows_times(first_block, other)
+            img[...] = rows_times(first_block, w)
+
+        def send_pieces(t):
+            @pl.when(jnp.logical_not(interior))
+            def _():
+                for piece in range(2):
+                    at = piece_rows(piece)
+                    zsend[t, at] = wrecv[t, at].astype(jnp.bfloat16)
+                    scatter(t, piece).start()
+
+        def forward_piece(t, piece):
+            @pl.when(interior)
+            def _():
+                block = target_block(t)
+                arrived(block, piece).wait()
+                at = piece_rows(piece)
+                total = wrecv[t, at] + zrecv[block, at].astype(jnp.float32)
+                zsend[t, at] = total.astype(jnp.bfloat16)
+                scatter(t, piece).start()
+
+        def forwards(unit):
+            for t in range(n_lb - 1):
+                if unit == min(2 * t + 2, units - 1):
+                    forward_piece(t, 0)
+                if unit == min(2 * t + 3, units):
+                    forward_piece(t, 1)
+
+        exchange(0).start()
+        exchange(0).wait_recv()
+        wrecv[0] = wrecv[0] + img[...]
+        send_pieces(0)
+        for t in range(1, n_lb):
             block = target_block(t)
-
-            @pl.when(it == 0)
-            def _():
-                load_block(t).wait()
-
+            loaded(t)
             wsend[t] = rows_times(block, other)
             exchange(t).start()
+            forwards(2 * t - 1)
             value = rows_times(block, w)
             exchange(t).wait_recv()
-            return value + wrecv[t]
-
-        def away(t, c):
-            zsend[t] = block_sum(t).astype(jnp.bfloat16)
-            scatter(t).start()
-            return c
-
-        lax.fori_loop(0, n_lb - 1, away, 0)
-        img[...] = block_sum(n_lb - 1)
+            if t < n_lb - 1:
+                wrecv[t] = value + wrecv[t]
+                send_pieces(t)
+            else:
+                img[...] = value + wrecv[t]
+            forwards(2 * t)
 
         @pl.when(it == 0)
         def _():
@@ -380,23 +477,43 @@
         for t in range(n_lb):
             exchange(t).wait_send()
         for t in range(n_lb - 1):
-            scatter(t).wait_send()
-        for t in range(n_lb - 1):
-            scatter(t).wait_recv()
+            for piece in range(2):
+                scatter(t, piece).wait_send()
+
+        @pl.when(it > 0)
+        def _():
+            for n, value in enumerate(reduce_finish(0, ITERS)):
+                over[n] = value
+
+        @pl.when(i > 0)
+        def _():
+            for piece in range(2):
+                arrived(i, piece).wait()
+
+        @pl.when(i < n_lb - 1)
+        def _():
+            for piece in range(2):
+                arrived(n_lb, piece).wait()
 
         def measure(c, sums):
             at = rows_at(c * chunk)
-            y = img[at, :]
-            for t in range(n_lb - 1):
-                y = y + zrecv[t, at, :].astype(jnp.float32)
+            y = img[at, :] + (
+                zrecv[i, at, :].astype(jnp.float32) + zrecv[n_lb, at, :].astype(jnp.float32)
+            )
+            x = vec[at, :]
+            members = [basis[n, at, :] for n in range(ITERS)]
+            for n in range(ITERS):
+                overlap = scalar_of(over[n])
+                x = x - overlap * members[n]
+                y = y - overlap * images[n, at, :]
+            vec[at, :] = x
             img[at, :] = y
-            x = vec[at, :]
-            parts = [x * x, x * y] + [basis[n, at, :] * y for n in range(ITERS)]
+            parts = [x * x, x * y] + [member * y for member in members]
             return tuple(total + fold(part) for total, part in zip(sums, parts))
 
         zero = jnp.zeros(TILE, jnp.float32)
-        sums = over_chunks(measure, (zero,) * (2 + ITERS))
-        sums = all_reduce(1, sums)
+        reduce_start(1, over_chunks(measure, (zero,) * (2 + ITERS)))
+        sums = reduce_finish(1, 2 + ITERS)
         scale = lax.rsqrt(sums[0] + epsilon)
 
         def keep(c, carry):
@@ -437,25 +554,14 @@
                 value, _, r = ritz(at, ITERS)
                 x = r / (jnp.abs(diag[at, :] - value) + 1.0)
                 vec[at, :] = x
+                xall[j, w, at, :] = x.astype(jnp.bfloat16)
                 return tuple(
                     total + fold(basis[n, at, :] * x) for n, total in enumerate(sums)
                 )
 
-            overlaps = all_reduce(0, over_chunks(correct, (zero,) * ITERS))
-
-            def project(c, carry):
-                at = rows_at(c * chunk)
-                x = vec[at, :]
-                total = scalar_of(overlaps[0]) * basis[0, at, :]
-                for n in range(1, ITERS):
-                    total = total + scalar_of(overlaps[n]) * basis[n, at, :]
-                x = x - total
-                vec[at, :] = x
-                xall[j, w, at, :] = x.astype(jnp.bfloat16)
-                return carry
-
-            over_chunks(project, 0)
+            overlaps = over_chunks(correct, (zero,) * ITERS)
             send_vector()
+            reduce_start(0, overlaps)
 
         @pl.when(it == ITERS)
         def _():
@@ -530,7 +636,7 @@
             pltpu.VMEM((n_lb, half, width), f32),
             pltpu.VMEM((n_lb, half, width), f32),
             pltpu.VMEM((n_lb - 1, half, width), bf16),
-            pltpu.VMEM((n_lb - 1, half, width), bf16),
+            pltpu.VMEM((n_lb + 1, half, width), bf16),
             pltpu.VMEM((members, half, width), f32),
             pltpu.VMEM((members, half, width), f32),
             pltpu.VMEM((half, width), f32),
@@ -540,6 +646,7 @@
             pltpu.VMEM((2, devices, 1, LANES), f32),
             pltpu.VMEM((members * members,) + TILE, f32),
             pltpu.VMEM((members + 1,) + TILE, f32),
+            pltpu.VMEM((ITERS,) + TILE, f32),
             dma((n_lb,)),
             dma((n_rb,)),
             dma((n_rb,)),
@@ -547,8 +654,8 @@
             dma((n_rb,)),
             dma((n_lb,)),
             dma((n_lb,)),
-            dma((n_lb,)),
-            dma((n_lb,)),
+            dma((2 * n_lb,)),
+            dma((2 * n_lb + 2,)),
             dma((2,)),
             dma((2,)),
             dma((2,)),

time: 256 us -> 228 us (0.89)
  Pallas kernels: 244 us -> 216 us
    pallas_call x1, Pallas kernels: 244 us -> 216 us  [per_device(): pl.pallas_call(functools.partial(davidson_kernel, dims), out_shape=(outs,...]
where the time goes in v1:
time: 228 us
  Pallas kernels  216 us (95%)
  local copies, waits for them, and re-layouts  7.69 us (3%)
    pallas_call x1, Pallas kernels, per_device(): pl.pallas_call(functools.partial(davidson_kernel, dims), out_shape=(outs,...  216 us
    reshape x2, local copies, waits for them, and re-layouts, per_device(): return (vectors.reshape(shape), residuals.reshape(shape))  5.06 us

profile of v1, /device:TPU:0, one launch (start us, length us, event | category | flops | bytes accessed | tf_op | source)
XLA Modules:
  0.0 228.0 jit_solution(7068719157897328586)
XLA Ops:
  0.6 0.0 copy-start
  0.6 0.8 slice_bitcast_fusion.1
  1.4 1.4 convolution_bitcast_fusion
  2.8 0.3 copy.10
  3.1 0.8 reshape.19.op_ref
  3.9 0.0 copy-done
  3.9 0.1 constant_dynamic-slice_fusion
  4.0 0.7 copy.20
  4.7 1.8 convert_bitcast_fusion.right_ref
  6.5 216.5 %davidson.1 = (f32[512,512]{1,0:T(8,128)}, f32[512,512]{1,0:T(8,128)}) custom-call(f32[1024]{0:T(1024)} %reshape.19.op_ref, bf16[256,512]{1,0:T(8,128)(2,1)} %bitcast.29, f32[8,128,128]{2,1,0:T(8,128)} %convert_bitcast_fusion.right_ref, bf16[4,2048,2048]{2,1,0:T(8,128)(2,1)} %bitcast.28), custom_call_target="tpu_custom_call" | custom-call | tf_op jit(solution)/shard_map/davidson/pallas_call | solution.py:626
  223.0 2.5 %reshape.22 = f32[512,4,128]{2,1,0:T(4,128)} reshape(f32[512,512]{1,0:T(8,128)} %get-tuple-element.4) | data formatting | bytes 2097152 | tf_op jit(solution)/shard_map/reshape | solution.py:671
  225.5 2.5 %reshape.23 = f32[512,4,128]{2,1,0:T(4,128)} reshape(f32[512,512]{1,0:T(8,128)} %get-tuple-element.5) | data formatting | bytes 2097152 | tf_op jit(solution)/shard_map/reshape | solution.py:671
  (1 shorter events, 0.0 us)
Async XLA Ops:
  0.6 3.2 %copy-start = (bf16[512,4,128]{2,1,0:T(4,128)(2,1)S(1)}, bf16[512,4,128]{2,1,0:T(4,128)(2,1)}, u32[]{:S(2)}) copy-start(bf16[512,4,128]{2,1,0:T(4,128)(2,1)} %param.5) | copy-start | bytes 1572868

commit v2 on v1

--- a/solution.py
+++ b/solution.py
@@ -80,11 +80,13 @@
 
 
 def dense_operator(operator_blocks, operator_pairs, levels):
+    blocks, physical, _ = operator_blocks.shape
+    square = physical * physical
     symmetric = 0.5 * (operator_blocks + jnp.swapaxes(operator_blocks, 1, 2))
-    indices = jnp.arange(levels, dtype=jnp.int32)
-    left_hot = (operator_pairs[:, 0:1] == indices[None, :]).astype(jnp.float32)
-    right_hot = (operator_pairs[:, 1:2] == indices[None, :]).astype(jnp.float32)
-    return jnp.einsum("nw,nv,nts->wvts", left_hot, right_hot, symmetric, precision=highest)
+    entries = symmetric.reshape(blocks, 1, square)
+    place = lax.broadcasted_iota(jnp.int32, (1, levels * levels, 1), 1)
+    wanted = operator_pairs[:, 0] * levels + operator_pairs[:, 1]
+    return jnp.sum(jnp.where(place == wanted[:, None, None], entries, 0.0), axis=0)
 
 
 def fold(block):
@@ -106,7 +108,7 @@
     op_ref, guess_ref, right_ref, left_hbm,
     vec_out, res_out,
     left, joint, xall, inner, wsend, wrecv, zsend, zrecv,
-    basis, images, diag, vec, img, rows_ref, dots, sub, pair, over,
+    basis, images, diag, vec, img, rows_ref, dots, sub, pair, over, sizes, right_f32, out3,
     load_sem, gx_send, gx_recv, gw_send, gw_recv, w_send, w_recv, z_send, z_recv,
     d_sem, dot_send, dot_recv, out_sem,
 ):
@@ -195,6 +197,8 @@
     over_chunks(prepare, 0)
     for n in range(ITERS):
         over[n] = jnp.zeros(TILE, jnp.float32)
+    for n in range(ITERS + 1):
+        sizes[n] = jnp.zeros(TILE, jnp.float32)
 
     @pl.when(i == 0)
     def _():
@@ -206,36 +210,61 @@
 
     pl.semaphore_wait(barrier, devices - 1)
 
-    def gather_rb(step):
-        q = rb_step(step, 1)
+    relayed = rb_major == 2 and rb_minor == 2
+    direct = range(1, 3) if relayed else range(1, n_rb)
+    quarter = half // 2
+
+    def piece_rows(piece):
+        return pl.ds(piece * quarter, quarter)
+
+    def gather_rb(step, piece):
+        q, at = rb_step(step, 1), piece_rows(piece)
         return remote(
-            xall.at[j, w], xall.at[j, w], gx_send.at[step], gx_recv.at[step], (i, q, w)
+            xall.at[j, w, at], xall.at[j, w, at], gx_send.at[2 * step + piece],
+            gx_recv.at[2 * step + piece], (i, q, w),
         )
 
-    def gather_wa(step):
-        q = rb_step(step, -1)
-        return remote(xall.at[q, w], xall.at[q, w], gw_send.at[step], gw_recv.at[step], partner)
+    def relay(piece):
+        source, onward = rb_step(2 - w, -1), rb_step(1 + w, 1)
+        at = piece_rows(piece)
+        return remote(
+            xall.at[source, w, at], xall.at[source, w, at], gx_send.at[6 + piece],
+            gx_recv.at[6 + piece], (i, onward, w),
+        )
+
+    def gathered(step, piece):
+        mine = xall.at[rb_step(step, -1), w, piece_rows(piece)]
+        return pltpu.make_async_copy(mine, mine, gx_recv.at[2 * step + piece])
+
+    def gather_wa(step, piece):
+        q, at = rb_step(step, -1), piece_rows(piece)
+        return remote(
+            xall.at[q, w, at], xall.at[q, w, at], gw_send.at[2 * step + piece],
+            gw_recv.at[2 * step + piece], partner,
+        )
 
     def send_vector():
-        gather_wa(0).start()
-        for step in range(1, n_rb):
-            gather_rb(step).start()
+        for piece in range(2):
+            for step in direct:
+                gather_rb(step, piece).start()
+            gather_wa(0, piece).start()
 
     send_vector()
 
-    op_base = w * (local_levels * levels * physical * physical)
+    right_f32[...] = right_ref[...].astype(jnp.float32)
+
+    op_base = w * (local_levels * levels)
     band = min(32, window)
 
     def make_joint(index, carry):
         k = lax.div(index, window // band)
         r0 = lax.rem(index, window // band) * band
-        mats = [right_ref[v, pl.ds(pl.multiple_of(r0, band), band), :] for v in range(levels)]
+        mats = [right_f32[pl.ds(pl.multiple_of(r0, band), band), v, :] for v in range(levels)]
         for s in range(physical):
             for t in range(physical):
                 total = None
                 for v in range(levels):
-                    at = op_base + ((k * levels + v) * physical + t) * physical + s
-                    term = op_ref[at] * mats[v]
+                    term = op_ref[op_base + k * levels + v, t * physical + s] * mats[v]
                     total = term if total is None else total + term
                 high = total.astype(jnp.bfloat16)
                 low = (total - high.astype(jnp.float32)).astype(jnp.bfloat16)
@@ -250,14 +279,13 @@
         jnp.int32, (window, window), 1
     )
     right_diag = [
-        jnp.sum(jnp.where(eye, right_ref[v], 0.0), axis=0, keepdims=True) for v in range(levels)
+        jnp.sum(jnp.where(eye, right_f32[:, v, :], 0.0), axis=0, keepdims=True) for v in range(levels)
     ]
     for k in range(local_levels):
         for s in range(physical):
             total = None
             for v in range(levels):
-                at = op_base + ((k * levels + v) * physical + s) * physical + s
-                term = op_ref[at] * right_diag[v]
+                term = op_ref[op_base + k * levels + v, s * physical + s] * right_diag[v]
                 total = term if total is None else total + term
             rows_ref[k, :, s * window : (s + 1) * window] = total
 
@@ -322,6 +350,21 @@
 
         lax.fori_loop(0, local_levels, one, 0)
 
+    def inner_pieces(blocks, u, piece):
+        x = jnp.concatenate([xall[q, u, piece_rows(piece)] for q in blocks], axis=0)
+
+        def one(k, carry):
+            value = jnp.dot(x, joint[k, 0], preferred_element_type=jnp.float32)
+            value = value + jnp.dot(x, joint[k, 1], preferred_element_type=jnp.float32)
+            value = value.astype(jnp.bfloat16)
+            for n, q in enumerate(blocks):
+                first = q * own_rows + u * half + piece * quarter
+                at = pl.ds(pl.multiple_of(first, quarter), quarter)
+                inner[k, at, :] = value[n * quarter : (n + 1) * quarter]
+            return carry
+
+        lax.fori_loop(0, local_levels, one, 0)
+
     def rows_times(block, u):
         at = pl.ds(pl.multiple_of(block * own_rows + u * half, half), half)
         total = None
@@ -344,9 +387,6 @@
     def exchange(t):
         return remote(wsend.at[t], wrecv.at[t], w_send.at[t], w_recv.at[t], partner)
 
-    def piece_rows(piece):
-        return pl.ds(piece * (half // 2), half // 2)
-
     def scatter(t, piece):
         block = target_block(t)
         right = block > i
@@ -376,31 +416,63 @@
         first_block = target_block(0)
         loaded(0)
 
-        def first_parts(q, start):
+        def first_parts(q, start, last):
             if not by_parts:
                 return
             for u, dst in ((other, wsend.at[0]), (w, img)):
                 value = rows_times_part(first_block, u, q)
                 dst[...] = value if start else dst[...] + value
+                if u is other and last is not False:
+
+                    @pl.when(last)
+                    def _():
+                        exchange(0).start()
 
         inner_block(j, w)
-        gather_wa(0).wait_recv()
+        for piece in range(2):
+            gather_wa(0, piece).wait_recv()
         inner_block(j, other)
-        first_parts(j, True)
+        first_parts(j, True, n_rb == 1)
 
         def arrive(step, c):
             q = rb_step(step, -1)
-            gather_rb(step).wait_recv()
-            gather_wa(step).start()
+            for piece in range(2):
+                gathered(step, piece).wait()
+                gather_wa(step, piece).start()
             inner_block(q, w)
-            gather_wa(step).wait_recv()
+            for piece in range(2):
+                gather_wa(step, piece).wait_recv()
             inner_block(q, other)
-            first_parts(q, False)
+            first_parts(q, False, step == n_rb - 1)
             return c
 
-        lax.fori_loop(1, n_rb, arrive, 0)
+        if relayed:
+            near = [rb_step(1, -1), rb_step(2, -1)]
+            far = rb_step(3, -1)
+            for piece in range(2):
+                for step in direct:
+                    gathered(step, piece).wait()
+                relay(piece).start()
+                for step in direct:
+                    gather_wa(step, piece).start()
+                inner_pieces(near, w, piece)
+                for step in direct:
+                    gather_wa(step, piece).wait_recv()
+                inner_pieces(near, other, piece)
+            for piece in range(2):
+                first_parts(near[piece], False, False)
+                gathered(3, piece).wait()
+                gather_wa(3, piece).start()
+            inner_block(far, w)
+            for piece in range(2):
+                gather_wa(3, piece).wait_recv()
+            inner_block(far, other)
+            first_parts(far, False, True)
+        else:
+            lax.fori_loop(1, n_rb, arrive, 0)
         if not by_parts:
             wsend[0] = rows_times(first_block, other)
+            exchange(0).start()
             img[...] = rows_times(first_block, w)
 
         def send_pieces(t):
@@ -428,7 +500,6 @@
                 if unit == min(2 * t + 3, units):
                     forward_piece(t, 1)
 
-        exchange(0).start()
         exchange(0).wait_recv()
         wrecv[0] = wrecv[0] + img[...]
         send_pieces(0)
@@ -470,10 +541,13 @@
 
             over_chunks(join, 0)
 
-        gather_wa(0).wait_send()
-        for step in range(1, n_rb):
-            gather_rb(step).wait_send()
-            gather_wa(step).wait_send()
+        for piece in range(2):
+            for step in direct:
+                gather_rb(step, piece).wait_send()
+            for step in range(n_rb):
+                gather_wa(step, piece).wait_send()
+            if relayed:
+                relay(piece).wait_send()
         for t in range(n_lb):
             exchange(t).wait_send()
         for t in range(n_lb - 1):
@@ -483,7 +557,7 @@
         @pl.when(it > 0)
         def _():
             for n, value in enumerate(reduce_finish(0, ITERS)):
-                over[n] = value
+                over[n] = value * sizes[n] * sizes[n]
 
         @pl.when(i > 0)
         def _():
@@ -506,8 +580,8 @@
                 overlap = scalar_of(over[n])
                 x = x - overlap * members[n]
                 y = y - overlap * images[n, at, :]
-            vec[at, :] = x
-            img[at, :] = y
+            basis[it, at, :] = x
+            images[it, at, :] = y
             parts = [x * x, x * y] + [member * y for member in members]
             return tuple(total + fold(part) for total, part in zip(sums, parts))
 
@@ -516,13 +590,7 @@
         sums = reduce_finish(1, 2 + ITERS)
         scale = lax.rsqrt(sums[0] + epsilon)
 
-        def keep(c, carry):
-            at = rows_at(c * chunk)
-            basis[it, at, :] = vec[at, :] * scalar_of(scale)
-            images[it, at, :] = img[at, :] * scalar_of(scale)
-            return carry
-
-        over_chunks(keep, 0)
+        sizes[it] = scale
 
         for order in range(1, ITERS + 2):
 
@@ -530,12 +598,12 @@
             def _():
                 last = order - 1
                 for n in range(last):
-                    sub[n * (ITERS + 1) + last] = sums[2 + n] * scale
+                    sub[n * (ITERS + 1) + last] = sums[2 + n] * sizes[n] * scale
                 sub[last * (ITERS + 1) + last] = sums[1] * scale * scale
                 value, weights = lowest_pair(order, lambda a, b: sub[a * (ITERS + 1) + b])
                 pair[0] = value
                 for n in range(ITERS + 1):
-                    pair[n + 1] = weights[n] if n < order else zero
+                    pair[n + 1] = weights[n] * sizes[n] if n < order else zero
 
         def ritz(at, members):
             value = scalar_of(pair[0])
@@ -568,18 +636,19 @@
             def finish(c, carry):
                 at = rows_at(c * chunk)
                 _, u, r = ritz(at, ITERS + 1)
-                vec[at, :] = u
-                img[at, :] = r
+                for s in range(physical):
+                    out3[0, at, s, :] = u[:, s * window : (s + 1) * window]
+                    out3[1, at, s, :] = r[:, s * window : (s + 1) * window]
                 return carry
 
             over_chunks(finish, 0)
             span = pl.ds(pl.multiple_of(w * half, half), half)
             moves = []
-            for n, (src, dst) in enumerate(((vec, vec_out), (img, res_out))):
+            for n, (src, dst) in enumerate(((out3.at[0], vec_out), (out3.at[1], res_out))):
                 moves.append(
-                    remote(src, dst.at[span, :], out_sem.at[3 * n], out_sem.at[3 * n + 1], partner)
+                    remote(src, dst.at[span], out_sem.at[3 * n], out_sem.at[3 * n + 1], partner)
                 )
-                moves.append(pltpu.make_async_copy(src, dst.at[span, :], out_sem.at[3 * n + 2]))
+                moves.append(pltpu.make_async_copy(src, dst.at[span], out_sem.at[3 * n + 2]))
             for move in moves:
                 move.start()
             for move in moves:
@@ -609,8 +678,7 @@
     total_count = own_rows * physical * window * n_lb * n_rb
     devices = n_lb * n_rb * n_wa
 
-    operator = dense_operator(operator_blocks, operator_pairs, levels).reshape(-1)
-    right = jnp.transpose(right_environment, (1, 0, 2)).astype(jnp.float32)
+    operator = dense_operator(operator_blocks, operator_pairs, levels)
     left_matrix = left_environment.reshape(local_levels, coarse * own_rows, contracted)
     guess = lax.dynamic_slice_in_dim(initial_guess, lax.axis_index("wa") * half, half, 0)
     guess = guess.reshape(half, width)
@@ -620,10 +688,10 @@
     f32, bf16 = jnp.float32, jnp.bfloat16
     members = ITERS + 1
     dma = pltpu.SemaphoreType.DMA
-    outs = jax.ShapeDtypeStruct((own_rows, width), f32)
+    outs = jax.ShapeDtypeStruct((own_rows, physical, window), f32)
     vmem = pl.BlockSpec(memory_space=pltpu.VMEM)
     hbm = pl.BlockSpec(memory_space=pl.ANY)
-    vectors, residuals = pl.pallas_call(
+    return pl.pallas_call(
         functools.partial(davidson_kernel, dims),
         out_shape=(outs, outs),
         in_specs=[pl.BlockSpec(memory_space=pltpu.SMEM), vmem, vmem, hbm],
@@ -647,11 +715,14 @@
             pltpu.VMEM((members * members,) + TILE, f32),
             pltpu.VMEM((members + 1,) + TILE, f32),
             pltpu.VMEM((ITERS,) + TILE, f32),
+            pltpu.VMEM((members,) + TILE, f32),
+            pltpu.VMEM((window, levels, window), f32),
+            pltpu.VMEM((2, half, physical, window), f32),
             dma((n_lb,)),
-            dma((n_rb,)),
-            dma((n_rb,)),
-            dma((n_rb,)),
-            dma((n_rb,)),
+            dma((2 * n_rb,)),
+            dma((2 * n_rb,)),
+            dma((2 * n_rb,)),
+            dma((2 * n_rb,)),
             dma((n_lb,)),
             dma((n_lb,)),
             dma((2 * n_lb,)),
@@ -665,10 +736,7 @@
             collective_id=0, has_side_effects=True, vmem_limit_bytes=VMEM_BYTES
         ),
         name="davidson",
-    )(operator, guess, right, left_matrix)
-
-    shape = (own_rows, physical, window)
-    return vectors.reshape(shape), residuals.reshape(shape)
+    )(operator, guess, right_environment, left_matrix)
 
 
 def solution(mesh):

time: 228 us -> 240 us (1.053)
  Pallas kernels: 216 us -> 232 us
    pallas_call x1, Pallas kernels: 216 us -> 232 us  [per_device(): pl.pallas_call(functools.partial(davidson_kernel, dims), out_shape=(outs,...]
    reshape x3 -> x0, local copies, waits for them, and re-layouts: 5.82 us -> none  [the longest x2 5.06 us: per_device(): return (vectors.reshape(shape), residuals.reshape(shape))]
    unnamed x3 -> x5, local copies, waits for them, and re-layouts: 0.75 us -> 5.27 us
where the time goes in v2:
time: 240 us
  Pallas kernels  232 us (97%)
  local copies, waits for them, and re-layouts  6.14 us (3%)
    pallas_call x1, Pallas kernels, per_device(): pl.pallas_call(functools.partial(davidson_kernel, dims), out_shape=(outs,...  232 us
    unnamed x5, local copies, waits for them, and re-layouts  5.27 us

profile of v2, /device:TPU:0, one launch (start us, length us, event | category | flops | bytes accessed | tf_op | source)
XLA Modules:
  0.0 240.0 jit_solution(882387023887424121)
XLA Ops:
  0.6 0.0 copy-start
  0.6 0.8 add_bitcast_fusion
  1.4 0.1 iota_compare_fusion
  1.5 0.8 fusion
  2.3 0.1 copy.10
  2.3 0.1 select_reduce_fusion
  2.4 0.7 copy.11.op_ref
  3.1 0.0 copy-done
  3.1 0.1 constant_dynamic-slice_fusion
  3.2 0.7 copy.15
  4.0 231.5 %davidson.1 = (f32[512,4,128]{2,1,0:T(4,128)}, f32[512,4,128]{2,1,0:T(4,128)}) custom-call(f32[64,16]{1,0:T(8,128)} %copy.11.op_ref, bf16[256,512]{1,0:T(8,128)(2,1)} %bitcast.13, bf16[128,8,128]{2,1,0:T(8,128)(2,1)} %right_ref.1, bf16[4,2048,2048]{2,1,0:T(8,128)(2,1)} %bitcast.12), custom_call_target="tpu_custom_call" | custom-call | tf_op jit(solution)/shard_map/davidson/pallas_call | solution.py:694
  235.5 2.3 copy.18
  237.8 2.3 copy.19
Async XLA Ops:
  0.6 2.5 %copy-start = (bf16[512,4,128]{2,1,0:T(4,128)(2,1)S(1)}, bf16[512,4,128]{2,1,0:T(4,128)(2,1)}, u32[]{:S(2)}) copy-start(bf16[512,4,128]{2,1,0:T(4,128)(2,1)} %param.5) | copy-start | bytes 1572868
